TPU v7x, 32 devices: a whole 2x2x4 slice. The times are simulated.
32 devices in a mesh: query: 4 (over y, x), train: 4 (over z), mp: 2 (over core).
Axes of the slice: x: 2, y: 2, z: 4, core: 2. Of those that a mesh axis runs over, the one named last changes fastest.
Arguments:
- residual: bfloat16 [512, 8192], P('train'), may hold values from -6 to 6
- norm_gain: float32 [8192], replicated, may hold values from 0.1 to 1.9
- gate_weight: bfloat16 [8192, 14336], P('train', ('query', 'mp')), may hold values from -0.0625 to 0.0625
- up_weight: bfloat16 [8192, 14336], P('train', ('query', 'mp')), may hold values from -0.0625 to 0.0625
- out_grad: bfloat16 [512, 8192], P('train', ('query', 'mp')), may hold values from -6 to 6
- left_factor: bfloat16 [8, 32, 14336], P(('query', 'mp')), may hold values from -0.0078125 to 0.0078125
- right_factor: bfloat16 [8, 32, 8192], P(('query', 'mp')), may hold values from -0.0625 to 0.0625
Outputs:
- scores: float32 [8, 512], P(('query', 'mp'), 'train')
All inputs are finite; a program needn't handle non-finite values.
Results may differ from a plain program's by a relative error of at most 0.023.
Values may be sent and summed in bfloat16 or wider, within the bound.
A program may use at most 64 MiB of HBM per device.

v0:
```python
import jax
import jax.numpy as jnp
from jax import lax
from jax.sharding import PartitionSpec as P

norm_eps = 1e-05


def on_device(residual, norm_gain, gate_weight, up_weight, out_grad, left_factor, right_factor):
    values = residual.astype(jnp.float32)
    mean_sq = jnp.mean(values * values, axis=1, keepdims=True)
    normed = (values * lax.rsqrt(mean_sq + norm_eps) * norm_gain[None, :]).astype(jnp.bfloat16)
    tok_rows = normed.shape[0]
    hidden_cols = gate_weight.shape[1]
    all_rows = lax.all_to_all(normed, "train", split_axis=1, concat_axis=0, tiled=True)
    paired = jnp.concatenate([gate_weight, up_weight], axis=1)
    summed = lax.psum_scatter(
        jnp.dot(all_rows, paired, preferred_element_type=jnp.float32).astype(jnp.bfloat16),
        "train",
        scatter_dimension=0,
        tiled=True,
    ).astype(jnp.float32)
    activation = (jax.nn.silu(summed[:, :hidden_cols]) * summed[:, hidden_cols:]).astype(
        jnp.bfloat16
    )
    queries = left_factor.shape[0]
    factor_rank = left_factor.shape[1]
    contract = (((1,), (1,)), ((), ()))
    left_flat = left_factor.reshape(queries * factor_rank, left_factor.shape[2])
    columns = left_flat
    projected = lax.dot_general(
        columns,
        lax.all_gather(activation, ("query", "mp"), axis=1, tiled=True),
        contract,
        preferred_element_type=jnp.float32,
    )
    right_flat = right_factor.reshape(queries * factor_rank, right_factor.shape[2])
    columns = right_flat
    sensed = lax.dot_general(
        columns,
        lax.all_gather(out_grad, ("query", "mp"), axis=1, tiled=True),
        contract,
        preferred_element_type=jnp.float32,
    )
    return jnp.sum((projected * sensed).reshape(queries, factor_rank, tok_rows), axis=1)


def solution(mesh):
    placed = (
        P("train", None),
        P(),
        P("train", ("query", "mp")),
        P("train", ("query", "mp")),
        P("train", ("query", "mp")),
        P(("query", "mp"), None, None),
        P(("query", "mp"), None, None),
    )
    return jax.shard_map(
        on_device,
        mesh=mesh,
        in_specs=placed,
        out_specs=P(("query", "mp"), "train"),
        check_vma=False,
    )
```

profile of v0, /device:TPU:0, one launch (start us, length us, event | category | flops | bytes accessed | tf_op | source)
XLA Modules:
  0.0 204.0 jit_solution(16912763031052419279)
XLA Ops:
  7.4 0.0 copy-start
  7.4 0.0 copy-start.2
  7.4 0.0 reduce-scatter.2.cloned.1.call-start
  7.4 3.3 %copy.8 = bf16[128,8192]{0,1:T(8,128)(2,1)S(1)} copy(bf16[128,8192]{1,0:T(8,128)(2,1)} %param.7) | data formatting | bytes 4194304 | tf_op args[0]
  10.7 1.1 fusion.7
  11.8 0.0 copy-done.2
  11.8 3.5 %fusion.9 = bf16[128,8192]{0,1:T(8,128)(2,1)S(1)} fusion(bf16[128,8192]{0,1:T(8,128)(2,1)S(1)} %copy.8, f32[8192]{0:T(1024)S(1)} %copy-done.2, f32[128]{0:T(128)S(1)} %add_rsqrt_fusion), kind=kLoop, calls=%fused_computation.9 | loop fusion | flops 4194304 | bytes 4227584 | tf_op jit(solution)/shard_map/convert_element_type | solution.py:12
  15.3 54.3 %all_to_all.19 = bf16[128,4,2048]{0,2,1:T(8,128)(2,1)S(1)} all-to-all(bf16[128,4,2048]{0,2,1:T(8,128)(2,1)S(1)} %bitcast.19), channel_id=1, replica_groups=mesh['query'=4,'train'=4,'mp'=2] {'train'}, dimensions={1} | all-to-all | bytes 4194304 | tf_op jit(solution)/shard_map/all_to_all | solution.py:15
  69.6 2.7 %copy.9 = bf16[4,128,2048]{2,1,0:T(8,128)(2,1)} copy(bf16[4,128,2048]{1,2,0:T(8,128)(2,1)S(1)} %bitcast.20) | data formatting | bytes 4194304 | tf_op jit(solution)/shard_map/all_to_all | solution.py:15
  72.3 15.3 %fusion.4 = bf16[512,3584]{1,0:T(8,128)(2,1)} fusion(bf16[512,2048]{1,0:T(8,128)(2,1)} %bitcast.21, bf16[2048,1792]{1,0:T(8,128)(2,1)} %param.10, bf16[2048,1792]{1,0:T(8,128)(2,1)} %param.9), kind=kOutput, calls=%fused_computation.4 | convolution fusion | flops 7547387904 | bytes 20447232 | tf_op jit(solution)/shard_map/dot_general | solution.py:18
  87.6 0.0 reduce-scatter.2.cloned.1.call-update
  87.7 0.0 copy-start.1
  87.7 0.0 all-gather.5.cloned.1.call-start
  87.7 0.5 all-gather.5.cloned.1.call-update
  88.3 0.0 all-gather.3.cloned.1.call-start
  88.3 67.3 %reduce-scatter.2.cloned.1.call-done = bf16[128,3584]{1,0:T(8,128)(2,1)} async-done(((bf16[512,3584]{1,0:T(8,128)(2,1)}), bf16[128,3584]{1,0:T(8,128)(2,1)}) %reduce-scatter.2.cloned.1.call-update) | async-done | bytes 917520 | tf_op jit(solution)/shard_map/reduce_scatter | solution.py:17
  155.6 1.4 convert_element_type.18
  157.0 1.0 fusion.12
  158.0 0.0 all-gather.3.cloned.1.call-update
  158.0 0.0 all-gather.5.cloned.1.call-done
  158.1 0.0 copy-done.1
  158.1 2.4 %fusion.14 = f32[32,128]{1,0:T(8,128)S(1)} fusion(bf16[128,8192]{1,0:T(8,128)(2,1)} %all-gather.5.cloned.1.call-done, bf16[1,32,8192]{2,1,0:T(8,128)(2,1)S(1)} %copy-done.1), kind=kOutput, calls=%fused_computation.16 | convolution fusion | flops 67108864 | bytes 2637824 | tf_op jit(solution)/shard_map/dot_general | solution.py:39
  160.5 32.2 %all-gather.3.cloned.1.call-done = bf16[128,14336]{1,0:T(8,128)(2,1)} async-done(((bf16[128,1792]{1,0:T(8,128)(2,1)}), bf16[128,14336]{1,0:T(8,128)(2,1)}) %all-gather.3.cloned.1.call-update) | async-done | bytes 3670032 | tf_op jit(solution)/shard_map/all_gather | solution.py:33
  192.6 0.0 copy-done
  192.7 3.9 %fusion.11 = f32[128]{0:T(128)} fusion(f32[32,128]{1,0:T(8,128)S(1)} %fusion.14, bf16[128,14336]{1,0:T(8,128)(2,1)} %all-gather.3.cloned.1.call-done, bf16[1,32,14336]{2,1,0:T(8,128)(2,1)S(1)} %copy-done), kind=kOutput, calls=%fused_computation.12 | convolution fusion | flops 117448576 | bytes 4604416 | tf_op jit(solution)/shard_map/dot_general | solution.py:31
  (1 shorter events, 0.0 us)
Async XLA Ops:
  7.4 185.3 %copy-start = (bf16[1,32,14336]{2,1,0:T(8,128)(2,1)S(1)}, bf16[1,32,14336]{2,1,0:T(8,128)(2,1)}, u32[]{:S(2)}) copy-start(bf16[1,32,14336]{2,1,0:T(8,128)(2,1)} %param.12) | copy-start | bytes 2752516
  7.4 4.4 %copy-start.2 = (f32[8192]{0:T(1024)S(1)}, f32[8192]{0:T(1024)}, u32[]{:S(2)}) copy-start(f32[8192]{0:T(1024)} %param.8) | copy-start | bytes 98308
  7.4 148.2 %reduce-scatter.2.cloned.1.call-start = ((), (), s32[]{:S(2)}) async-start(), calls=%async_computation.2 | async-start | bytes 4587520 | tf_op jit(solution)/shard_map/reduce_scatter | solution.py:17
  87.7 70.4 %copy-start.1 = (bf16[1,32,8192]{2,1,0:T(8,128)(2,1)S(1)}, bf16[1,32,8192]{2,1,0:T(8,128)(2,1)}, u32[]{:S(2)}) copy-start(bf16[1,32,8192]{2,1,0:T(8,128)(2,1)} %param.13) | copy-start | bytes 1572868
  87.7 70.4 %all-gather.5.cloned.1.call-start = ((), (), s32[]{:S(2)}) async-start(), calls=%async_computation.4 | async-start | bytes 2359296 | tf_op jit(solution)/shard_map/all_gather | solution.py:41
  88.3 104.4 %all-gather.3.cloned.1.call-start = ((), (), s32[]{:S(2)}) async-start(), calls=%async_computation.3 | async-start | bytes 4128768 | tf_op jit(solution)/shard_map/all_gather | solution.py:33
Sparse Core Ops, SparseCore 0:
  87.8 67.7 reduce-scatter.1
Sparse Core Ops, SparseCore 1:
  90.1 26.9 all-gather.4
  158.1 34.5 all-gather.2
where the time goes:
time: 204 us
  waiting for transfers between devices  100 us (49%)
  blocking collectives  54.3 us (27%)
  matrix products  21.6 us (11%)
  between operations  14.9 us (7%)
  other arithmetic  6.99 us (3%)
  local copies, waits for them, and re-layouts  6 us (3%)
    reduce_scatter x1, waiting for transfers between devices, on_device(): lax.psum_scatter(jnp.dot(all_rows, paired, preferred_element_type=jnp.flo...  67.3 us
    all_to_all x1, blocking collectives, on_device(): lax.all_to_all(normed, 'train', split_axis=1, concat_axis=0, tiled=True)  54.3 us
    all_gather x1, waiting for transfers between devices, on_device(): lax.all_gather(activation, ('query', 'mp'), axis=1, tiled=True)  32.2 us
    dot_general x1, matrix products, on_device(): jnp.dot(all_rows, paired, preferred_element_type=jnp.float32)  15.3 us
  transfers between devices with their start and end apart: 3, of which 2 were waited for; matrix products, arithmetic and copies ran while one was open for 2% of the time, Pallas kernels for 0%

commit v1 on v0

--- a/solution.py
+++ b/solution.py
@@ -12,7 +12,9 @@
     normed = (values * lax.rsqrt(mean_sq + norm_eps) * norm_gain[None, :]).astype(jnp.bfloat16)
     tok_rows = normed.shape[0]
     hidden_cols = gate_weight.shape[1]
-    all_rows = lax.all_to_all(normed, "train", split_axis=1, concat_axis=0, tiled=True)
+    pieces = jnp.split(normed, lax.axis_size("train"), axis=1)
+    received = lax.all_to_all(jnp.stack(pieces), "train", 0, 0)
+    all_rows = jnp.concatenate(received, axis=0)
     paired = jnp.concatenate([gate_weight, up_weight], axis=1)
     summed = lax.psum_scatter(
         jnp.dot(all_rows, paired, preferred_element_type=jnp.float32).astype(jnp.bfloat16),

time: 204 us -> 198 us (0.971)
  local copies, waits for them, and re-layouts: 6 us -> 0.25 us
    unnamed x7 -> x4, local copies, waits for them, and re-layouts: 3.32 us -> 0.01 us
    all_to_all x1 -> x0, local copies, waits for them, and re-layouts: 2.68 us -> none  [on_device(): lax.all_to_all(normed, 'train', split_axis=1, concat_axis=0, tiled=True)]
where the time goes in v1:
time: 198 us
  waiting for transfers between devices  100 us (51%)
  blocking collectives  54.3 us (27%)
  matrix products  21 us (11%)
  between operations  14.9 us (8%)
  other arithmetic  7 us (4%)
    reduce_scatter x1, waiting for transfers between devices, on_device(): lax.psum_scatter(jnp.dot(all_rows, paired, preferred_element_type=jnp.flo...  67.3 us
    all_to_all x1, blocking collectives, on_device(): received = lax.all_to_all(jnp.stack(pieces), 'train', 0, 0)  54.3 us
    all_gather x1, waiting for transfers between devices, on_device(): lax.all_gather(activation, ('query', 'mp'), axis=1, tiled=True)  32.1 us
    dot_general x1, matrix products, on_device(): jnp.dot(all_rows, paired, preferred_element_type=jnp.float32)  14.7 us
  transfers between devices with their start and end apart: 3, of which 2 were waited for; matrix products, arithmetic and copies ran while one was open for 2% of the time, Pallas kernels for 0%

profile of v1, /device:TPU:0, one launch (start us, length us, event | category | flops | bytes accessed | tf_op | source)
XLA Modules:
  0.0 197.6 jit_solution(10406666988058493172)
XLA Ops:
  7.4 0.0 copy-start
  7.4 0.0 reduce-scatter.2.cloned.1.call-start
  7.4 2.2 %fusion.7 = f32[128]{0:T(128)S(1)} fusion(bf16[128,8192]{1,0:T(8,128)(2,1)} %param.7), kind=kLoop, calls=%fused_computation.7 | loop fusion | flops 3145600 | bytes 2097664 | tf_op jit(solution)/shard_map/reduce_sum | solution.py:11
  9.5 2.2 %fusion.9 = bf16[128,8192]{1,0:T(8,128)(2,1)S(1)} fusion(bf16[128,8192]{1,0:T(8,128)(2,1)} %param.7, f32[8192]{0:T(1024)} %param.8, f32[128]{0:T(128)S(1)} %add_rsqrt_fusion), kind=kLoop, calls=%fused_computation.9 | loop fusion | flops 4194304 | bytes 4227584 | tf_op jit(solution)/shard_map/convert_element_type | solution.py:12
  11.7 0.2 slice_bitcast_fusion.3
  12.0 0.3 pad_maximum_fusion
  12.2 54.3 %all_to_all.5 = bf16[4,128,2048]{2,1,0:T(8,128)(2,1)S(1)} all-to-all(bf16[4,128,2048]{2,1,0:T(8,128)(2,1)S(1)} %pad_maximum_fusion), channel_id=1, replica_groups=mesh['query'=4,'train'=4,'mp'=2] {'train'}, dimensions={0} | all-to-all | bytes 4194304 | tf_op jit(solution)/shard_map/all_to_all | solution.py:16
  66.6 14.7 %fusion.4 = bf16[512,3584]{1,0:T(8,128)(2,1)} fusion(bf16[512,2048]{1,0:T(8,128)(2,1)S(1)} %bitcast.25, bf16[2048,1792]{1,0:T(8,128)(2,1)} %param.10, bf16[2048,1792]{1,0:T(8,128)(2,1)} %param.9), kind=kOutput, calls=%fused_computation.4 | convolution fusion | flops 7547387904 | bytes 20447232 | tf_op jit(solution)/shard_map/dot_general | solution.py:20
  81.3 0.0 reduce-scatter.2.cloned.1.call-update
  81.3 0.0 copy-start.1
  81.3 0.0 all-gather.5.cloned.1.call-start
  81.4 0.5 all-gather.5.cloned.1.call-update
  81.9 0.0 all-gather.3.cloned.1.call-start
  82.0 67.3 %reduce-scatter.2.cloned.1.call-done = bf16[128,3584]{1,0:T(8,128)(2,1)} async-done(((bf16[512,3584]{1,0:T(8,128)(2,1)}), bf16[128,3584]{1,0:T(8,128)(2,1)}) %reduce-scatter.2.cloned.1.call-update) | async-done | bytes 917520 | tf_op jit(solution)/shard_map/reduce_scatter | solution.py:19
  149.3 1.4 convert_element_type.18
  150.6 1.0 fusion.12
  151.7 0.0 all-gather.3.cloned.1.call-update
  151.7 0.0 all-gather.5.cloned.1.call-done
  151.7 0.0 copy-done.1
  151.7 2.4 %fusion.14 = f32[32,128]{1,0:T(8,128)S(1)} fusion(bf16[128,8192]{1,0:T(8,128)(2,1)} %all-gather.5.cloned.1.call-done, bf16[1,32,8192]{2,1,0:T(8,128)(2,1)S(1)} %copy-done.1), kind=kOutput, calls=%fused_computation.21 | convolution fusion | flops 67108864 | bytes 2637824 | tf_op jit(solution)/shard_map/dot_general | solution.py:41
  154.1 32.1 %all-gather.3.cloned.1.call-done = bf16[128,14336]{1,0:T(8,128)(2,1)} async-done(((bf16[128,1792]{1,0:T(8,128)(2,1)}), bf16[128,14336]{1,0:T(8,128)(2,1)}) %all-gather.3.cloned.1.call-update) | async-done | bytes 3670032 | tf_op jit(solution)/shard_map/all_gather | solution.py:35
  186.3 0.0 copy-done
  186.3 3.9 %fusion.11 = f32[128]{0:T(128)} fusion(f32[32,128]{1,0:T(8,128)S(1)} %fusion.14, bf16[128,14336]{1,0:T(8,128)(2,1)} %all-gather.3.cloned.1.call-done, bf16[1,32,14336]{2,1,0:T(8,128)(2,1)S(1)} %copy-done), kind=kOutput, calls=%fused_computation.13 | convolution fusion | flops 117448576 | bytes 4604416 | tf_op jit(solution)/shard_map/dot_general | solution.py:33
  (1 shorter events, 0.0 us)
Async XLA Ops:
  7.4 178.9 %copy-start = (bf16[1,32,14336]{2,1,0:T(8,128)(2,1)S(1)}, bf16[1,32,14336]{2,1,0:T(8,128)(2,1)}, u32[]{:S(2)}) copy-start(bf16[1,32,14336]{2,1,0:T(8,128)(2,1)} %param.12) | copy-start | bytes 2752516
  7.4 141.9 %reduce-scatter.2.cloned.1.call-start = ((), (), s32[]{:S(2)}) async-start(), calls=%async_computation.2 | async-start | bytes 4587520 | tf_op jit(solution)/shard_map/reduce_scatter | solution.py:19
  81.3 70.4 %copy-start.1 = (bf16[1,32,8192]{2,1,0:T(8,128)(2,1)S(1)}, bf16[1,32,8192]{2,1,0:T(8,128)(2,1)}, u32[]{:S(2)}) copy-start(bf16[1,32,8192]{2,1,0:T(8,128)(2,1)} %param.13) | copy-start | bytes 1572868
  81.3 70.4 %all-gather.5.cloned.1.call-start = ((), (), s32[]{:S(2)}) async-start(), calls=%async_computation.4 | async-start | bytes 2359296 | tf_op jit(solution)/shard_map/all_gather | solution.py:43
  81.9 104.4 %all-gather.3.cloned.1.call-start = ((), (), s32[]{:S(2)}) async-start(), calls=%async_computation.3 | async-start | bytes 4128768 | tf_op jit(solution)/shard_map/all_gather | solution.py:35
Sparse Core Ops, SparseCore 0:
  81.4 67.7 reduce-scatter.1
Sparse Core Ops, SparseCore 1:
  83.7 26.9 all-gather.4
  151.8 34.5 all-gather.2
